TPU v7x, 32 devices: a whole 2x2x4 slice. The times are simulated.
32 devices in a mesh: seq: 8 (over z, x), head: 4 (over y, core).
Axes of the slice: x: 2, y: 2, z: 4, core: 2. Of those that a mesh axis runs over, the one named last changes fastest.
Arguments:
- queries: bfloat16 [8192, 4096], P('seq', 'head'), may hold values from -150 to 150
- keys: bfloat16 [8192, 4096], P('seq', 'head'), may hold values from -7 to 7
- values: bfloat16 [8192, 4096], P('seq', 'head'), may hold values from -6 to 6
- random_holder: int32 [32, 64, 3], P('head', 'seq'), may hold values from 0 to 7, all different within a row; in each aligned block of 8 rows (0 to 7, 8 to 15, ..., all dimensions but the last counted through in order) at most 3 rows name the same one
- random_offset: int32 [32, 64, 3], P('head', 'seq'), may hold values from 0 to 7
- keep: int32 [64], P('seq'), may hold values from 0 to 1, as said below
Outputs:
- packed: bfloat16 [8192, 4096], P('seq', 'head')
Inputs may be any that keep to these rules, and one draw needn't show every extreme that they name: `random_holder`: for each head, the 8 query blocks of one index of seq name no index of seq more than 3 times over all their random entries; the 3 entries of one query block and head differ. `keep`: block j is kept where j % 8 == 0 or j % 8 == 7, and not kept where j % 8 == 1.
All inputs are finite; a program needn't handle non-finite values.
Results may differ from a plain program's by a relative error of at most 0.007.
Values may be sent and summed in bfloat16 or wider, within the bound.
A program may use at most 128 MiB of HBM per device.

v0:
```python
import functools
import math

import jax
import jax.numpy as jnp
from jax import lax
from jax.experimental import pallas as pl
from jax.experimental.pallas import tpu as pltpu
from jax.sharding import PartitionSpec as P

DH = 128
B = 128
G = 2
R = 3

neg_big = -1e30
ANYWHERE = pltpu.CompilerParams(
    dimension_semantics=("arbitrary",), vmem_limit_bytes=60 * 1024 * 1024
)


def halo(block, axis, width):
    count = lax.axis_size(axis)
    forward = [(i, i + 1) for i in range(count - 1)]
    backward = [(target, source) for source, target in forward]
    low = lax.ppermute(block[-width:], axis, forward)
    high = lax.ppermute(block[:width], axis, backward)
    return jnp.concatenate([low, high], axis=0)


def broadcast(block, axis, source):
    block = jnp.where(lax.axis_index(axis) == source, block, jnp.zeros_like(block))
    return lax.psum(block, axis)


def pick_kernel(cap, head_ref, block_ref, k_ref, v_ref, out_ref):
    dest = pl.program_id(0)

    @pl.loop(0, cap)
    def _(j):
        rows = pl.ds(pl.multiple_of(block_ref[dest, j] * B, B), B)
        cols = pl.ds(pl.multiple_of(head_ref[dest, j] * DH, DH), DH)
        out_ref[j, 0] = k_ref[rows, cols]
        out_ref[j, 1] = v_ref[rows, cols]


def pick(keys, values, heads, blocks, seq_count, cap):
    whole = pl.BlockSpec(keys.shape, lambda d, *_: (0, 0))
    return pl.pallas_call(
        functools.partial(pick_kernel, cap),
        out_shape=jax.ShapeDtypeStruct((seq_count * cap, 2, B, DH), keys.dtype),
        grid_spec=pltpu.PrefetchScalarGridSpec(
            num_scalar_prefetch=2,
            grid=(seq_count,),
            in_specs=[whole, whole],
            out_specs=pl.BlockSpec((cap, 2, B, DH), lambda d, *_: (d, 0, 0, 0)),
        ),
        compiler_params=ANYWHERE,
    )(heads, blocks, keys, values)


def attend_kernel(
    blk_dev,
    keep_ref,
    slot_ref,
    live_ref,
    where_ref,
    q_ref,
    k_ref,
    v_ref,
    hk_ref,
    hv_ref,
    gk_ref,
    gv_ref,
    rand_ref,
    out_ref,
):
    scale = 1.0 / math.sqrt(DH)
    head = pl.program_id(0)
    out_ref[...] = jnp.zeros_like(out_ref)

    def tile(ref, halo_ref, i):
        if i < 0:
            return halo_ref[:B]
        if i >= blk_dev:
            return halo_ref[B:]
        return ref[i * B : (i + 1) * B]

    def one(i):
        q = q_ref[i * B : (i + 1) * B]
        near = range(i - 1, i + 2)
        picks = [where_ref[(head * blk_dev + i) * R + r] for r in range(R)]
        k_parts = [
            jnp.concatenate([tile(k_ref, hk_ref, n) for n in near], axis=0),
            gk_ref[...],
            jnp.concatenate([rand_ref[p, 0] for p in picks], axis=0),
        ]
        v_parts = [
            jnp.concatenate([tile(v_ref, hv_ref, n) for n in near], axis=0),
            gv_ref[...],
            jnp.concatenate([rand_ref[p, 1] for p in picks], axis=0),
        ]
        scores = [
            lax.dot_general(
                q, k, (((1,), (1,)), ((), ())), preferred_element_type=jnp.float32
            )
            * scale
            for k in k_parts
        ]
        lanes = lax.broadcasted_iota(jnp.int32, scores[0].shape, 1)
        if i == 0:
            dead = jnp.logical_and(lanes < B, live_ref[0] == 0)
            scores[0] = jnp.where(dead, neg_big, scores[0])
        if i == blk_dev - 1:
            dead = jnp.logical_and(lanes >= 2 * B, live_ref[1] == 0)
            scores[0] = jnp.where(dead, neg_big, scores[0])
        peak = functools.reduce(
            jnp.maximum, [jnp.max(s, axis=-1, keepdims=True) for s in scores]
        )
        numer = jnp.zeros((B, DH), jnp.float32)
        denom = jnp.zeros((B, 1), jnp.float32)
        for s, v in zip(scores, v_parts):
            w = jnp.exp(s - peak).astype(jnp.bfloat16)
            denom = denom + jnp.sum(w.astype(jnp.float32), axis=-1, keepdims=True)
            numer = numer + jnp.dot(w, v, preferred_element_type=jnp.float32)
        rows = pl.ds(pl.multiple_of(slot_ref[i] * B, B), B)
        out_ref[rows, :] = (numer / denom).astype(out_ref.dtype)

    for i in range(blk_dev):
        pl.when(keep_ref[i] > 0)(functools.partial(one, i))


def attend(keep, slot, live, where, q, k, v, hk, hv, gk, gv, rand):
    tok_dev, width_dev = q.shape
    blk_dev, head_dev = tok_dev // B, width_dev // DH

    def column(rows):
        return pl.BlockSpec((rows, DH), lambda h, *_: (0, h))

    return pl.pallas_call(
        functools.partial(attend_kernel, blk_dev),
        out_shape=jax.ShapeDtypeStruct(q.shape, q.dtype),
        grid_spec=pltpu.PrefetchScalarGridSpec(
            num_scalar_prefetch=4,
            grid=(head_dev,),
            in_specs=[column(tok_dev)] * 3
            + [column(2 * B)] * 2
            + [column(G * B)] * 2
            + [pl.BlockSpec(rand.shape, lambda h, *_: (0, 0, 0, 0))],
            out_specs=column(tok_dev),
        ),
        compiler_params=ANYWHERE,
    )(keep, slot, live, where, q, k, v, hk, hv, gk, gv, rand)


def copy_kernel(order_ref, in_ref, out_ref):
    out_ref[...] = in_ref[...]


def take_blocks(blocks, order, cap):
    width = blocks.shape[1]
    return pl.pallas_call(
        copy_kernel,
        out_shape=jax.ShapeDtypeStruct((cap * B, width), blocks.dtype),
        grid_spec=pltpu.PrefetchScalarGridSpec(
            num_scalar_prefetch=1,
            grid=(cap,),
            in_specs=[pl.BlockSpec((B, width), lambda j, order: (order[j], 0))],
            out_specs=pl.BlockSpec((B, width), lambda j, order: (j, 0)),
        ),
        compiler_params=ANYWHERE,
    )(order, blocks)


def merge_kernel(kind_ref, from_ref, old_ref, new_ref, out_ref):
    kind = kind_ref[pl.program_id(0)]

    @pl.when(kind == 0)
    def _():
        out_ref[...] = old_ref[...]

    @pl.when(kind == 1)
    def _():
        out_ref[...] = jnp.zeros_like(out_ref)

    @pl.when(kind == 2)
    def _():
        out_ref[...] = new_ref[...]


def merge_blocks(old, new, kind, place):
    tok_dev, width = old.shape
    return pl.pallas_call(
        merge_kernel,
        out_shape=jax.ShapeDtypeStruct(old.shape, old.dtype),
        grid_spec=pltpu.PrefetchScalarGridSpec(
            num_scalar_prefetch=2,
            grid=(tok_dev // B,),
            in_specs=[
                pl.BlockSpec((B, width), lambda j, kind, place: (j, 0)),
                pl.BlockSpec((B, width), lambda j, kind, place: (place[j], 0)),
            ],
            out_specs=pl.BlockSpec((B, width), lambda j, kind, place: (j, 0)),
        ),
        compiler_params=ANYWHERE,
    )(kind, place, old, new)


def exclusive(flags, axis):
    return jnp.cumsum(flags, axis=axis) - flags


def first_at_least(caps, amount):
    return jnp.sum((amount > jnp.asarray(caps, jnp.int32)).astype(jnp.int32))


def settle(blocks, keep_all, slot, source, distance, me, count, blk_dev):
    i32 = jnp.int32
    devices = jnp.arange(count, dtype=i32)
    slots = jnp.arange(blk_dev, dtype=i32)
    sizes = sorted({0, *range(blk_dev // 2, blk_dev - 1), blk_dev})
    for bit_pos in range((count - 1).bit_length()):
        stride = 2**bit_pos
        at = source - distance % stride
        moving = (keep_all > 0) & (distance // stride % 2 > 0)
        on_slot = ((slot[:, None] == slots) & moving[:, None]).astype(i32)
        on_device = (at[:, None] == devices).astype(i32)
        leaving = jnp.sum(on_device[:, :, None] * on_slot[:, None, :], axis=0)
        needed = jnp.max(jnp.sum(leaving, axis=1))
        nth = exclusive(leaving, 1)
        mine_out, mine_nth = leaving[me], nth[me]
        send = jnp.sum(
            mine_out[:, None] * (mine_nth[:, None] == slots).astype(i32) * slots[:, None], axis=0
        )
        far = jnp.minimum(me + stride, count - 1)
        comes = jnp.where(me + stride < count, leaving[far], 0)
        kind = jnp.where(comes > 0, 2, jnp.where(mine_out > 0, 1, 0)).astype(i32)
        place = jnp.where(comes > 0, nth[far], 0)
        all_pairs = [(i, i - stride) for i in range(stride, count)]
        split = count - stride // 2
        upper = [pair for pair in all_pairs if pair[0] >= split]
        halves = 2 * stride >= count and 0 < len(upper) < len(all_pairs)

        def shifting(cap, pairs, send=send, kind=kind, place=place):
            def run(blocks):
                if cap == 0:
                    return blocks
                moved = lax.ppermute(take_blocks(blocks, send, cap), "seq", pairs)
                return merge_blocks(blocks, moved, kind, jnp.minimum(place, cap - 1))

            return run

        which = first_at_least(sizes[:-1], needed)
        runs = [shifting(cap, all_pairs) for cap in sizes]
        if halves:
            runs += [shifting(cap, upper) for cap in sizes]
            lower = jnp.sum(leaving * (devices < split)[:, None].astype(i32))
            which = which + jnp.where(lower > 0, 0, len(sizes))
        blocks = lax.switch(which, runs, blocks)
    return blocks


def plain_body(queries, keys, values, random_holder, random_offset, keep):
    tok_dev, width_dev = queries.shape
    blk_dev = tok_dev // B
    head_dev = width_dev // DH
    seq_count = lax.axis_size("seq")
    head_count = lax.axis_size("head")
    me = lax.axis_index("seq")
    count_req = blk_dev * R
    total = head_dev * count_req
    i32 = jnp.int32

    code = random_holder * blk_dev + random_offset
    code = jnp.where((keep > 0)[None, :, None], code, -1).reshape(total)
    note = jnp.concatenate([code, keep])
    note = jnp.broadcast_to(note, (seq_count * head_count,) + note.shape)
    table = lax.all_to_all(note, ("seq", "head"), split_axis=0, concat_axis=0, tiled=True)
    table = table.reshape(seq_count, head_count, total + blk_dev)
    keep_all = table[:, 0, total:].reshape(seq_count * blk_dev)
    codes = table[:, :, :total]
    devices = jnp.arange(seq_count, dtype=i32)

    halo_k, halo_v = halo(keys, "seq", B), halo(values, "seq", B)

    named = jnp.where(codes >= 0, codes // blk_dev, -1)
    counts = jnp.sum((named[..., None] == devices).astype(i32), axis=2)
    most = jnp.max(counts)
    onehot = (named[me, lax.axis_index("head")][:, None] == devices).astype(i32)
    mine = exclusive(onehot, 0)
    my_slot = jnp.sum(mine * onehot, axis=1)
    my_holder = jnp.sum(onehot * devices, axis=1)

    group = codes[:, lax.axis_index("head")]
    asks = (named[:, lax.axis_index("head")] == me).astype(i32)
    order = exclusive(asks, 1)
    full = min(total, head_dev * max(2, (count_req + seq_count - 1) // seq_count))
    chosen = asks[..., None] * (order[..., None] == jnp.arange(full, dtype=i32)).astype(i32)
    ask_head = jnp.arange(total, dtype=i32) // count_req
    ask = jnp.where(group >= 0, group % blk_dev, 0) + ask_head[None] * blk_dev
    ask = jnp.sum(chosen * ask[..., None], axis=1)
    pick_head, pick_block = ask // blk_dev, ask % blk_dev

    rank = exclusive(keep_all, 0)
    slot = rank % blk_dev
    source = jnp.arange(seq_count * blk_dev, dtype=i32) // blk_dev
    distance = jnp.where(keep_all > 0, source - rank // blk_dev, 0)
    my_slots = lax.dynamic_slice_in_dim(slot, me * blk_dev, blk_dev)
    live = jnp.stack([me > 0, me < seq_count - 1]).astype(i32)

    caps = sorted({max(1, full * part // 12) for part in range(8, 13)})

    def gathered(cap):
        def run(q, k, v, hk, hv):
            gk, gv = broadcast(jnp.stack((k[: G * B], v[: G * B])), "seq", 0)
            picked = pick(k, v, pick_head, pick_block, seq_count, cap)
            replies = lax.all_to_all(picked, "seq", split_axis=0, concat_axis=0, tiled=True)
            where = jnp.minimum(my_holder * cap + my_slot, seq_count * cap - 1)
            return attend(keep, my_slots, live, where, q, k, v, hk, hv, gk, gv, replies)

        return run

    blocks = lax.switch(
        first_at_least(caps[:-1], most),
        [gathered(cap) for cap in caps],
        queries, keys, values, halo_k, halo_v,
    )

    return settle(blocks, keep_all, slot, source, distance, me, seq_count, blk_dev)


TILE = (2 * B, DH)
SMALL = pltpu.CompilerParams(vmem_limit_bytes=60 * 1024 * 1024)


def fits(planes, tiles, most):
    slots = 2 * (planes - 1) * tiles + 2 * planes * most + most
    return slots * 2 * B * DH * 2 <= 44 * 1024 * 1024


def exchange_kernel(
    count, cz, cx, blk_dev, tab, k_ref, v_ref,
    rand_ref, halo_ref, glob_ref, home, zs, zr, xs, own,
    z_send, z_recv, x_send, x_recv, h_send, h_recv, g_send, g_recv, l_sem,
):
    planes = count // 2
    me = lax.axis_index("seq")
    plane, side = me // 2, me % 2
    mate = plane * 2 + 1 - side
    tok = k_ref.shape[0]
    head_dev = k_ref.shape[1] // DH
    barrier = pltpu.get_barrier_semaphore()
    for step in range(1, count):
        peer = lax.rem(me + step, count)
        pl.semaphore_signal(
            barrier, inc=1, device_id={"seq": peer}, device_id_type=pl.DeviceIdType.MESH
        )
    pl.semaphore_wait(barrier, count - 1)

    def remote(src, dst, send, recv, peer):
        return pltpu.make_async_remote_copy(
            src_ref=src, dst_ref=dst, send_sem=send, recv_sem=recv,
            device_id={"seq": peer}, device_id_type=pl.DeviceIdType.MESH,
        )

    tables = (k_ref, v_ref)
    low, high = pl.ds(0, B), pl.ds(B, B)
    first, last = pl.ds(0, B), pl.ds(tok - B, B)
    after = jnp.minimum(me + 1, count - 1)
    before = jnp.maximum(me - 1, 0)
    ups = [
        remote(tables[i].at[last], halo_ref.at[i, low], h_send.at[i], h_recv.at[i], after)
        for i in range(2)
    ]
    downs = [
        remote(tables[i].at[first], halo_ref.at[i, high], h_send.at[2 + i], h_recv.at[2 + i], before)
        for i in range(2)
    ]
    local = [
        pltpu.make_async_copy(tables[i].at[pl.ds(0, G * B)], glob_ref.at[i], l_sem.at[i])
        for i in range(2)
    ]
    item = glob_ref.at[side]
    chain = remote(item, item, g_send.at[0], g_recv.at[0], jnp.minimum(me + 2, count - 1))
    swap = remote(item, item, g_send.at[1], g_recv.at[1], mate)
    extra = remote(glob_ref.at[1], glob_ref.at[1], g_send.at[2], g_recv.at[0], mate)

    @pl.when(me == 0)
    def _():
        for c in local:
            c.start()
        for c in local:
            c.wait()
        chain.start()
        extra.start()
        swap.start()

    def pass_on():
        @pl.when(me > 0)
        def _():
            chain.wait_recv()

            @pl.when(plane < planes - 1)
            def _():
                chain.start()

            @pl.when(me > 1)
            def _():
                swap.start()

    @pl.when(me < count - 1)
    def _():
        for c in ups:
            c.start()

    @pl.when(me > 0)
    def _():
        for c in downs:
            c.start()

    @pl.when(me == 0)
    def _():
        halo_ref[:, low, :] = jnp.zeros((2, B, k_ref.shape[1]), k_ref.dtype)

    @pl.when(me == count - 1)
    def _():
        halo_ref[:, high, :] = jnp.zeros((2, B, k_ref.shape[1]), k_ref.dtype)

    def load_home(block, carry):
        rows = pl.ds(pl.multiple_of(block * B, B), B)
        for h in range(head_dev):
            cols = slice(h * DH, (h + 1) * DH)
            home[h * blk_dev + block, low, :] = k_ref[rows, cols]
            home[h * blk_dev + block, high, :] = v_ref[rows, cols]
        return carry

    lax.fori_loop(0, blk_dev, load_home, 0)

    def from_slots(dst, src, table, row, cap):
        def one(j, carry):
            dst[j] = src[table[row, j]]
            return carry

        lax.fori_loop(0, cap, one, 0)

    deltas = range(1, planes)

    def goals(q):
        return sorted(deltas, key=lambda d: (abs((q + d) % planes - q), d))

    def arrival(q, d):
        source, half = (q - d) % planes, planes // 2
        if (source < half) == (q < half):
            return (0, abs(source - q))
        edges = (half - 1, half)
        return (1 if source in edges and q in edges else 2 if source not in edges else 3, d)

    def sources(q):
        return sorted(deltas, key=lambda d: arrival(q, d))

    x_base = (planes - 1) * cz
    z_copies = {
        d: remote(
            zs[d - 1], zr[d - 1], z_send.at[d - 1], z_recv.at[d - 1],
            lax.rem(plane + d, planes) * 2 + side,
        )
        for d in deltas
    }
    x_copies = [
        remote(
            xs[d], rand_ref.at[pl.ds(x_base + d * cx, cx)],
            x_send.at[d], x_recv.at[d], mate,
        )
        for d in range(planes)
    ]
    for d in deltas:
        from_slots(zs[d - 1], home, tab, d - 1, cz)
    from_slots(xs[0], home, tab, planes - 1, cx)
    for q in range(planes):
        @pl.when(plane == q)
        def _(q=q):
            order = goals(q)
            for n, d in enumerate(order):
                z_copies[d].start()
                if n == 0 and q == 0:
                    pass_on()

    x_copies[0].start()
    from_slots(own, home, tab, 2 * planes - 1, cx)
    keep_own = pltpu.make_async_copy(
        own, rand_ref.at[pl.ds(x_base + planes * cx, cx)], l_sem.at[2]
    )
    keep_own.start()
    outs = {
        d: pltpu.make_async_copy(
            zr[d - 1], rand_ref.at[pl.ds((d - 1) * cz, cz)], l_sem.at[2 + d]
        )
        for d in deltas
    }

    def forward(d):
        z_copies[d].wait_recv()
        outs[d].start()
        from_slots(xs[d], zr[d - 1], tab, planes - 1 + d, cx)
        x_copies[d].start()

    for q in range(planes):
        @pl.when(plane == q)
        def _(q=q):
            for n, d in enumerate(sources(q)):
                forward(d)
                if n == 0 and 0 < q < planes // 2:
                    pass_on()
            if q >= planes // 2:
                pass_on()

    @pl.when(me > 0)
    def _():
        swap.wait_recv()

    @pl.when(plane < planes - 1)
    def _():
        chain.wait_send()

    @pl.when(me == 0)
    def _():
        extra.wait_send()

    @pl.when(me != 1)
    def _():
        swap.wait_send()

    @pl.when(me < count - 1)
    def _():
        for c in ups:
            c.wait_send()
        for c in downs:
            c.wait_recv()

    @pl.when(me > 0)
    def _():
        for c in downs:
            c.wait_send()
        for c in ups:
            c.wait_recv()

    keep_own.wait()
    for d in deltas:
        outs[d].wait()
        z_copies[d].wait_send()
    for c in x_copies:
        c.wait()


def exchange(count, level, cz, cx, slots, blk_dev, tab, keys, values):
    planes = count // 2
    tok, width = keys.shape
    smem = pl.BlockSpec(memory_space=pltpu.SMEM)
    vmem = pl.BlockSpec(memory_space=pltpu.VMEM)
    dtype = keys.dtype
    dma = pltpu.SemaphoreType.DMA
    return pl.pallas_call(
        functools.partial(exchange_kernel, count, cz, cx, blk_dev),
        out_shape=(
            jax.ShapeDtypeStruct((slots, *TILE), dtype),
            jax.ShapeDtypeStruct((2, 2 * B, width), dtype),
            jax.ShapeDtypeStruct((2, G * B, width), dtype),
        ),
        in_specs=[smem, vmem, vmem],
        out_specs=(pl.BlockSpec(memory_space=pl.ANY), vmem, vmem),
        scratch_shapes=[
            pltpu.VMEM((tok // B * (width // DH), *TILE), dtype),
            [pltpu.VMEM((cz, *TILE), dtype) for _ in range(planes - 1)],
            [pltpu.VMEM((cz, *TILE), dtype) for _ in range(planes - 1)],
            [pltpu.VMEM((cx, *TILE), dtype) for _ in range(planes)],
            pltpu.VMEM((cx, *TILE), dtype),
            dma((planes - 1,)), dma((planes - 1,)),
            dma((planes,)), dma((planes,)),
            dma((4,)), dma((4,)), dma((3,)), dma((2,)), dma((2 + planes,)),
        ],
        compiler_params=pltpu.CompilerParams(
            collective_id=level, has_side_effects=True,
            vmem_limit_bytes=60 * 1024 * 1024,
        ),
    )(tab, keys, values)


PIECES = 4


def settle_kernel(
    count, caps, cr, cx, blk_dev, table, in_ref, out_ref,
    mine, zs, pool, rs, xs, xr, z_send, z_recv, r_send, r_recv, x_send, x_recv,
):
    planes = count // 2
    me = lax.axis_index("seq")
    plane, side = me // 2, me % 2
    mate = plane * 2 + 1 - side
    wide = in_ref.shape[1] // PIECES
    barrier = pltpu.get_barrier_semaphore()
    for step in range(1, count):
        peer = lax.rem(me + step, count)
        pl.semaphore_signal(
            barrier, inc=1, device_id={"seq": peer}, device_id_type=pl.DeviceIdType.MESH
        )
    pl.semaphore_wait(barrier, count - 1)

    def remote(src, dst, send, recv, peer):
        return pltpu.make_async_remote_copy(
            src_ref=src, dst_ref=dst, send_sem=send, recv_sem=recv,
            device_id={"seq": peer}, device_id_type=pl.DeviceIdType.MESH,
        )

    used = [d for d in range(1, planes) if caps[d - 1] > 0]
    used.sort(reverse=True)
    base = {d: blk_dev + sum(caps[: d - 1]) for d in used}
    gate = planes // 2 - 1
    beyond = range(1, gate + 1)
    r_base = blk_dev + sum(caps)
    x_row = planes - 1 + max(gate, 1)

    def sends(d):
        return jnp.logical_and(plane >= d, jnp.logical_or(plane != gate + 1, d == 1))

    def gets(d):
        return jnp.logical_and(plane + d < planes, jnp.logical_or(plane + d != gate + 1, d == 1))

    def fill(dst, src, table, row, cap):
        def one(j, carry):
            dst[j] = src[table[row, j]]
            return carry

        lax.fori_loop(0, cap, one, 0)

    def own_part(piece):
        def one(j, carry):
            rows = pl.ds(pl.multiple_of(j * B, B), B)
            block = in_ref[rows, piece * wide : (piece + 1) * wide]
            mine[piece][j] = block
            pool[piece][j] = block
            return carry

        lax.fori_loop(0, blk_dev, one, 0)

    z_copies, x_copies = {}, []
    for piece in range(PIECES):
        for n, d in enumerate(used):
            z_copies[piece, d] = remote(
                zs[piece][n], pool[piece].at[pl.ds(base[d], caps[d - 1])],
                z_send.at[piece, n], z_recv.at[piece, n],
                jnp.maximum(me - 2 * d, 0),
            )
        for d in beyond:
            z_copies[piece, -d] = remote(
                rs[piece][d - 1], pool[piece].at[pl.ds(r_base, cr)],
                r_send.at[piece, d - 1], r_recv.at[piece],
                jnp.maximum(me - 2 * d, 0),
            )
        x_copies.append(remote(xs[piece], xr[piece], x_send.at[piece], x_recv.at[piece], mate))
    def start_z(piece):
        for d in used:
            @pl.when(sends(d))
            def _(d=d):
                z_copies[piece, d].start()

    for piece in range(PIECES):
        own_part(piece)
        for n, d in enumerate(used):
            fill(zs[piece][n], mine[piece], table, d - 1, caps[d - 1])
        if piece > 0:
            start_z(piece - 1)
    start_z(PIECES - 1)

    def finish(piece):
        x_copies[piece].wait_recv()

        def one(j, carry):
            rows = pl.ds(pl.multiple_of(j * B, B), B)
            kind = table[x_row + 1, j]
            near, far = pool[piece][table[x_row + 2, j]], xr[piece][table[x_row + 3, j]]
            block = jnp.where(kind == 1, near, jnp.where(kind == 2, far, jnp.zeros_like(far)))
            out_ref[rows, piece * wide : (piece + 1) * wide] = block
            return carry

        lax.fori_loop(0, blk_dev, one, 0)

    for piece in range(PIECES):
        for d in used:
            @pl.when(gets(d))
            def _(d=d, piece=piece):
                z_copies[piece, d].wait_recv()

        @pl.when(plane == gate)
        def _(piece=piece):
            for d in beyond:
                fill(rs[piece][d - 1], pool[piece], table, planes - 2 + d, cr)
                z_copies[piece, -d].start()

        @pl.when(plane < gate)
        def _(piece=piece):
            if gate > 0:
                z_copies[piece, -1].wait_recv()

        fill(xs[piece], pool[piece], table, x_row, cx)
        x_copies[piece].start()
        if piece > 0:
            finish(piece - 1)
    finish(PIECES - 1)
    for piece in range(PIECES):
        x_copies[piece].wait_send()
        for d in used:
            @pl.when(sends(d))
            def _(d=d, piece=piece):
                z_copies[piece, d].wait_send()

        @pl.when(plane == gate)
        def _(piece=piece):
            for d in beyond:
                z_copies[piece, -d].wait_send()


def settled(count, number, caps, cr, cx, blk_dev, packs, blocks):
    tok, width = blocks.shape
    planes, wide = count // 2, width // PIECES
    smem = pl.BlockSpec(memory_space=pltpu.SMEM)
    vmem = pl.BlockSpec(memory_space=pltpu.VMEM)
    dma, dtype = pltpu.SemaphoreType.DMA, blocks.dtype
    sent = [caps[d - 1] for d in range(planes - 1, 0, -1) if caps[d - 1] > 0]

    def each(rows):
        return [pltpu.VMEM((rows, B, wide), dtype) for _ in range(PIECES)]

    return pl.pallas_call(
        functools.partial(settle_kernel, count, caps, cr, cx, blk_dev),
        out_shape=jax.ShapeDtypeStruct(blocks.shape, dtype),
        in_specs=[smem, vmem],
        out_specs=vmem,
        scratch_shapes=[
            each(blk_dev),
            [[pltpu.VMEM((c, B, wide), dtype) for c in sent] for _ in range(PIECES)],
            each(blk_dev + sum(caps) + cr),
            [[pltpu.VMEM((cr, B, wide), dtype) for _ in range(planes // 2 - 1)] for _ in range(PIECES)],
            each(cx),
            each(cx),
            dma((PIECES, len(sent))), dma((PIECES, len(sent))),
            dma((PIECES, planes // 2)), dma((PIECES,)), dma((PIECES,)), dma((PIECES,)),
        ],
        compiler_params=pltpu.CompilerParams(
            collective_id=number, has_side_effects=True,
            vmem_limit_bytes=60 * 1024 * 1024,
        ),
    )(packs, blocks)


def settle_levels(planes, blk_dev):
    def pad(first, second):
        return ((first, second) + (0,) * planes)[: planes - 1]

    half, few = blk_dev // 2, blk_dev * 3 // 4
    choices = [
        (2 * max(f + t, f + r) + r, pad(f, t), r, few)
        for f in range(half, few + 1)
        for t in range(half, few + 1)
        for r in (half // 2, half)
        if abs(f - t) < 2 or t == half
    ]
    choices = sorted(choices) + [(0, (blk_dev,) * (planes - 1), blk_dev, blk_dev)]
    return [limits for _, *limits in choices]


def pack(blocks, packs, level, count, blk_dev, first_id, choices):
    def run(number, *limits):
        return lambda *args: settled(count, first_id + number, *limits, blk_dev, *args)

    runs = [run(n, *limits) for n, limits in enumerate(choices)]
    return lax.switch(level, runs, packs, blocks)


CHUNK = 8


def near_far_kernel(
    blk_dev, keep_ref, live_ref, where_ref, used_ref,
    q_ref, k_ref, v_ref, hk_ref, hv_ref, gk_ref, gv_ref, rand_hbm, out_ref, rand_ref, sems,
):
    scale = 1.0 / math.sqrt(DH)
    head = pl.program_id(0)
    chunks = rand_hbm.shape[0] // CHUNK

    @pl.when(head == 0)
    def _():
        def copy(c):
            rows = pl.ds(c * CHUNK, CHUNK)
            return pltpu.make_async_copy(rand_hbm.at[rows], rand_ref.at[rows], sems.at[c])

        for c in range(chunks):
            pl.when(c * CHUNK < used_ref[0, 1])(lambda c=c: copy(c).start())
        for c in range(chunks):
            pl.when(c * CHUNK < used_ref[0, 1])(lambda c=c: copy(c).wait())

    def tile(ref, halo_ref, i):
        if i < 0:
            return halo_ref[0, :B]
        if i >= blk_dev:
            return halo_ref[0, B:]
        return ref[i * B : (i + 1) * B]

    def one(i):
        q = q_ref[i * B : (i + 1) * B]
        near = range(i - 1, i + 2)
        picks = [where_ref[head, i * R + r] for r in range(R)]
        k_parts = [
            jnp.concatenate([tile(k_ref, hk_ref, n) for n in near], axis=0),
            gk_ref[0],
            jnp.concatenate([rand_ref[p, :B] for p in picks], axis=0),
        ]
        v_parts = [
            jnp.concatenate([tile(v_ref, hv_ref, n) for n in near], axis=0),
            gv_ref[0],
            jnp.concatenate([rand_ref[p, B:] for p in picks], axis=0),
        ]
        scores = [
            lax.dot_general(
                q, k, (((1,), (1,)), ((), ())), preferred_element_type=jnp.float32
            )
            * scale
            for k in k_parts
        ]
        lanes = lax.broadcasted_iota(jnp.int32, scores[0].shape, 1)
        if i == 0:
            dead = jnp.logical_and(lanes < B, live_ref[0] == 0)
            scores[0] = jnp.where(dead, neg_big, scores[0])
        if i == blk_dev - 1:
            dead = jnp.logical_and(lanes >= 2 * B, live_ref[1] == 0)
            scores[0] = jnp.where(dead, neg_big, scores[0])
        peak = functools.reduce(
            jnp.maximum, [jnp.max(s, axis=-1, keepdims=True) for s in scores]
        )
        numer = jnp.zeros((B, DH), jnp.float32)
        denom = jnp.zeros((B, 1), jnp.float32)
        for s, v in zip(scores, v_parts):
            w = jnp.exp(s - peak).astype(jnp.bfloat16)
            denom = denom + jnp.sum(w.astype(jnp.float32), axis=-1, keepdims=True)
            numer = numer + jnp.dot(w, v, preferred_element_type=jnp.float32)
        out_ref[i * B : (i + 1) * B, :] = (numer / denom).astype(out_ref.dtype)

    for i in range(blk_dev):
        pl.when(keep_ref[i] > 0)(functools.partial(one, i))


def near_far(keep, live, where, used, q, k, v, halo_kv, glob, rand):
    tok_dev, width_dev = q.shape
    blk_dev, head_dev = tok_dev // B, width_dev // DH

    def column(rows):
        return pl.BlockSpec((rows, DH), lambda h, *_: (0, h))

    def part(rows, which):
        return pl.BlockSpec((1, rows, DH), lambda h, *_: (which, 0, h))

    return pl.pallas_call(
        functools.partial(near_far_kernel, blk_dev),
        out_shape=jax.ShapeDtypeStruct(q.shape, q.dtype),
        grid_spec=pltpu.PrefetchScalarGridSpec(
            num_scalar_prefetch=4,
            grid=(head_dev,),
            in_specs=[column(tok_dev)] * 3
            + [part(2 * B, 0), part(2 * B, 1), part(G * B, 0), part(G * B, 1)]
            + [pl.BlockSpec(memory_space=pl.ANY)],
            out_specs=column(tok_dev),
            scratch_shapes=[
                pltpu.VMEM(rand.shape, rand.dtype),
                pltpu.SemaphoreType.DMA((rand.shape[0] // CHUNK,)),
            ],
        ),
        compiler_params=ANYWHERE,
    )(keep, live, where, used, q, k, v, halo_kv, halo_kv, glob, glob, rand)


def quotient(x, n):
    return jnp.floor((x.astype(jnp.float32) + 0.5) * (1.0 / n)).astype(jnp.int32)


def plan_kernel(
    count, head_count, blk_dev, most, caps, choices, note_ref, tab_ref, where_ref, misc_ref, pack_ref,
    need_ref, want_ref, slot_ref, both_ref, both_slot_ref,
):
    i32, f32, bf16 = jnp.int32, jnp.float32, jnp.bfloat16
    planes = count // 2
    me, group = lax.axis_index("seq"), lax.axis_index("head")
    plane, side = me // 2, me % 2
    mate = me + 1 - 2 * side
    rows, lanes = note_ref.shape[0], tab_ref.shape[1]
    head_dev = rows // (count * head_count)
    count_req = blk_dev * R
    blocks = count * blk_dev

    def iota(shape, axis):
        return lax.broadcasted_iota(i32, shape, axis)

    def dot(a, b):
        return jnp.dot(a.astype(bf16), b.astype(bf16), preferred_element_type=f32)

    def flag(x):
        return x.astype(f32)

    notes = note_ref[...]
    lane = iota((rows, lanes), 1)
    need = jnp.zeros((rows, lanes), f32)
    for e in range(count_req):
        need = jnp.where(notes[:, e : e + 1] == lane, 1.0, need)
    need_ref[...] = need

    wide_r, wide_c = iota((lanes, lanes), 0), iota((lanes, lanes), 1)
    own_r, own_c = quotient(wide_r, blk_dev), quotient(wide_c, blk_dev)
    same = flag(own_r == own_c)
    inside = flag((own_r == own_c) & (wide_r < wide_c))

    def by_head(x):
        return jnp.sum(x.reshape(-1, head_dev, lanes), axis=1)

    most_x = jnp.max(dot(by_head(need), same))
    span = head_count * head_dev
    pairs = need.reshape(planes, 2, span, lanes)
    union = jnp.maximum(pairs[:, 0], pairs[:, 1]).reshape(planes * span, lanes)
    union_count = dot(by_head(union), same)
    holder_plane = quotient(quotient(iota(union_count.shape, 1), blk_dev), 2)
    goal_plane = quotient(iota(union_count.shape, 0), head_count)
    most_z = jnp.max(jnp.where(holder_plane != goal_plane, union_count, 0.0))
    level = jnp.int32(0)
    cz, cx = jnp.int32(caps[0][0]), jnp.int32(caps[0][1])
    for n in range(1, len(caps)):
        over = (most_z > caps[n - 1][0]) | (most_x > caps[n - 1][1])
        level = jnp.where(over, n, level)
        cz = jnp.where(over, caps[n][0], cz)
        cx = jnp.where(over, caps[n][1], cx)

    for d in range(count):
        start = pl.multiple_of((d * head_count + group) * head_dev, head_dev)
        want_ref[d * head_dev : (d + 1) * head_dev, :] = need_ref[pl.ds(start, head_dev), :]
    want = want_ref[...]
    both = jnp.maximum(
        *[want.reshape(planes, 2, head_dev, lanes)[:, i] for i in range(2)]
    ).reshape(planes * head_dev, lanes)
    both_ref[...] = both

    def slots(x):
        tall = x.shape[0]
        r, c = iota((tall, tall), 0), iota((tall, tall), 1)
        above = flag((quotient(r, head_dev) == quotient(c, head_dev)) & (c < r))
        return dot(x, inside) + dot(above, dot(x, same))

    slot_ref[...] = slots(want)
    both_slot_ref[...] = slots(both)

    def head_rows(ref, i):
        return ref[pl.ds(pl.multiple_of(i * head_dev, head_dev), head_dev), :]

    def shifted(x, holder):
        return pltpu.roll(x, lax.rem(lanes - holder * blk_dev, lanes), 1)

    short = iota((head_dev, lanes), 1)
    first = iota((head_dev, 1), 0)

    def listed(flags, places, holder, worth):
        key = jnp.where(shifted(flags, holder) > 0, shifted(places, holder), -1.0).astype(i32)
        total = jnp.zeros((head_dev, lanes), f32)
        if worth is not None:
            worth = shifted(worth, holder)
        for b in range(blk_dev):
            value = (first * blk_dev + b).astype(f32) if worth is None else worth[:, b : b + 1]
            total = total + jnp.where(key[:, b : b + 1] == short, value, 0.0)
        return jnp.sum(total, axis=0, keepdims=True).astype(i32)

    tables = []
    for d in range(1, planes):
        goal = lax.rem(plane + d, planes)
        tables.append(listed(head_rows(both_ref, goal), head_rows(both_slot_ref, goal), me, None))
    here = head_rows(both_slot_ref, plane)
    for d in range(planes):
        source = lax.rem(plane - d + planes, planes) * 2 + side
        tables.append(
            listed(head_rows(want_ref, mate), head_rows(slot_ref, mate), source, here if d else None)
        )
    tables.append(listed(head_rows(want_ref, me), head_rows(slot_ref, me), me, None))
    tab_ref[...] = jnp.zeros(tab_ref.shape, i32)
    for n, row in enumerate(tables):
        tab_ref[n : n + 1, :] = row

    holder = quotient(short, blk_dev)
    h_plane = quotient(holder, 2)
    h_side = holder - 2 * h_plane
    gap = plane - h_plane
    gap = jnp.where(gap < 0, gap + planes, gap)
    x_base = (planes - 1) * cz
    by_z = (h_side == side) & (holder != me)
    start = jnp.where(
        by_z, (gap - 1) * cz, jnp.where(holder == me, x_base + planes * cx, x_base + gap * cx)
    )
    spot = start.astype(f32) + jnp.where(by_z, here, head_rows(slot_ref, me))
    mine = pl.multiple_of((me * head_count + group) * head_dev, head_dev)
    picks = note_ref[pl.ds(mine, head_dev), :]
    found = jnp.zeros((head_dev, lanes), f32)
    for e in range(count_req):
        value = jnp.sum(jnp.where(picks[:, e : e + 1] == short, spot, 0.0), axis=1, keepdims=True)
        found = jnp.where(short == e, value, found)
    where_ref[...] = found.astype(i32)

    grid_keep = note_ref[...].astype(f32)
    picked = jnp.zeros((count, grid_keep.shape[1]), f32)
    tall_r, tall_c = iota((count, rows), 0), iota((count, rows), 1)
    stride = head_count * head_dev
    picked = dot(flag(tall_c == tall_r * stride), jnp.clip(grid_keep, 0.0, 1.0))
    spread_r, spread_c = iota((picked.shape[1], lanes), 0), iota((picked.shape[1], lanes), 1)
    spread = flag(spread_r == count_req + spread_c - quotient(spread_c, blk_dev) * blk_dev)
    table = dot(picked, spread)
    row8, lane8 = iota((count, lanes), 0), iota((count, lanes), 1)
    kept_r = jnp.sum(jnp.where(quotient(lane8, blk_dev) == row8, table, 0.0), axis=0, keepdims=True)
    kept8 = jnp.broadcast_to(kept_r, (8, lanes))
    rank_r = dot(kept8, flag(wide_r < wide_c))[:1]

    sub, across = iota((blocks, lanes), 0), iota((blocks, lanes), 1)
    turn = sub == across

    def column(row):
        return jnp.sum(jnp.where(turn, row, 0.0), axis=1, keepdims=True)

    def facts(kept, rank, index):
        rank = rank.astype(i32)
        source, goal = quotient(index, blk_dev), quotient(rank, blk_dev)
        s_plane, g_plane = quotient(source, 2), quotient(goal, 2)
        gate = planes // 2 - 1
        relayed = (kept > 0) & (s_plane == gate + 1) & (g_plane < gate)
        far = jnp.where(relayed, 1, s_plane - g_plane)
        s_side, g_side = source - 2 * s_plane, goal - 2 * g_plane
        return kept > 0, rank, source, goal, g_plane, s_side, g_side, relayed, far

    index_r = iota((1, lanes), 1)
    index_c = iota((blocks, 1), 0)
    kr, _, sr, gr, pr, xr, yr, rr, fr = facts(kept_r, rank_r, index_r)
    kc, rank, sc, gc, pc, xc, yc, rc, fc = facts(column(kept_r), column(rank_r), index_c)
    earlier = across < sub

    def tally(hit):
        return jnp.sum(jnp.where(earlier & hit, 1.0, 0.0), axis=1, keepdims=True).astype(i32)

    by_z = tally((sc == sr) & (fc == fr) & kr)
    flow = (pc == pr) & (xc == xr)
    by_r = tally(flow & rr)
    by_x = tally(flow & kr & (xr != yr))
    crosses = kc & (xc != yc)
    gate = planes // 2 - 1

    def largest(hit, value):
        return jnp.max(jnp.where(hit, value + 1, 0).astype(f32))

    tops = [largest(kc & (fc == d), by_z) for d in range(1, planes)]
    top_r, top_x = largest(rc, by_r), largest(crosses, by_x)
    last = len(choices) - 1
    pick = jnp.int32(last)
    own = [jnp.int32(c) for c in choices[last][0]]
    for n in range(last - 1, -1, -1):
        limits, limit_r, limit_x = choices[n]
        ok = (top_r <= limit_r) & (top_x <= limit_x)
        for top, limit in zip(tops, limits):
            ok = ok & (top <= limit)
        pick = jnp.where(ok, n, pick)
        own = [jnp.where(ok, c, o) for c, o in zip(limits, own)]
    local = index_c - sc * blk_dev
    held = local
    base = jnp.int32(blk_dev)
    for d in range(1, planes):
        held = jnp.where(fc == d, base + by_z, held)
        base = base + own[d - 1]
    ahead = held
    held = jnp.where(rc, base + by_r, held)

    def rows_of(hit, places, worth):
        value = jnp.where(hit & (places == across), worth, 0).astype(f32)
        return jnp.sum(value, axis=0, keepdims=True).astype(i32)

    packs = [rows_of(kc & (fc == d) & (sc == me), by_z, local) for d in range(1, planes)]
    for d in range(1, max(gate, 1) + 1):
        packs.append(rows_of(rc & (xc == side) & (plane == gate) & (pc == gate - d), by_r, ahead))
    packs.append(rows_of(crosses & (pc == plane) & (xc == side), by_x, held))
    lands = kc & (gc == me)
    place = rank - gc * blk_dev
    straight = xc == side
    packs.append(rows_of(lands, place, jnp.where(straight, 1, 2)))
    packs.append(rows_of(lands & straight, place, held))
    packs.append(rows_of(lands & jnp.logical_not(straight), place, by_x))
    pack_ref[...] = jnp.zeros(pack_ref.shape, i32)
    for n, row in enumerate(packs):
        pack_ref[n : n + 1, :] = row

    used = x_base + (planes + 1) * cx
    spot8 = iota(misc_ref.shape, 1)
    misc_ref[...] = jnp.where(
        spot8 == 0, level, jnp.where(spot8 == 1, used, jnp.where(spot8 == 2, pick, 0))
    )


def plan(note, count, head_count, blk_dev, most, caps, choices):
    rows = note.shape[0]
    planes = count // 2
    head_dev = rows // (count * head_count)
    lanes = max(128, count * blk_dev)
    i32, f32 = jnp.int32, jnp.float32
    tabs = -(-2 * planes // 8) * 8
    packs = -(-(planes + max(planes // 2 - 1, 1) + 3) // 8) * 8
    shape = jax.ShapeDtypeStruct
    return pl.pallas_call(
        functools.partial(plan_kernel, count, head_count, blk_dev, most, caps, choices),
        out_shape=(
            shape((tabs, lanes), i32), shape((head_dev, lanes), i32),
            shape((8, lanes), i32), shape((packs, lanes), i32),
        ),
        scratch_shapes=[
            pltpu.VMEM((rows, lanes), f32),
            pltpu.VMEM((count * head_dev, lanes), f32), pltpu.VMEM((count * head_dev, lanes), f32),
            pltpu.VMEM((planes * head_dev, lanes), f32), pltpu.VMEM((planes * head_dev, lanes), f32),
        ],
        compiler_params=SMALL,
    )(note)


def levels(tiles, most):
    caps = []
    for part in (22, 24, 26, 28, 29, 30, 32, 36):
        cz = min(tiles, tiles * part // 64)
        caps.append((cz, min(most, max(1, most * min(24, part // 2 + 7) // 24))))
    caps.append((tiles, most))
    return sorted(set(caps))


def body(queries, keys, values, random_holder, random_offset, keep):
    tok_dev, width_dev = queries.shape
    blk_dev = tok_dev // B
    head_dev = width_dev // DH
    count = lax.axis_size("seq")
    head_count = lax.axis_size("head")
    count_req = blk_dev * R
    total = head_dev * count_req
    tiles = head_dev * blk_dev
    most = min(tiles, head_dev * max(2, (count_req + count - 1) // count))
    planes = count // 2
    if count % 2 or planes % 2 or not fits(planes, tiles, most):
        return plain_body(queries, keys, values, random_holder, random_offset, keep)
    me = lax.axis_index("seq")
    plane, side = me // 2, me % 2
    mate = me + 1 - 2 * side
    i32 = jnp.int32
    code = random_holder * blk_dev + random_offset
    code = jnp.where((keep > 0)[None, :, None], code, -1).reshape(head_dev, count_req)
    note = jnp.concatenate([code, jnp.broadcast_to(keep[None], (head_dev, blk_dev))], axis=1)
    note = jnp.broadcast_to(note, (count * head_count,) + note.shape)
    table = lax.all_to_all(note, ("seq", "head"), split_axis=0, concat_axis=0, tiled=True)
    table = table.reshape(count * head_count * head_dev, count_req + blk_dev)
    caps, choices = levels(tiles, most), settle_levels(planes, blk_dev)
    tab, where, misc, packs = plan(table, count, head_count, blk_dev, most, caps, choices)

    slots_all = -(-max((planes - 1) * c[0] + (planes + 1) * c[1] for c in caps) // CHUNK) * CHUNK
    def exchanged(number, caps):
        def run(tab, k, v):
            return exchange(count, number, *caps, slots_all, blk_dev, tab, k, v)

        return run

    rand, halo_kv, glob = lax.switch(
        misc[0, 0], [exchanged(n, c) for n, c in enumerate(caps)], tab, keys, values
    )

    live = jnp.stack([me > 0, me < count - 1]).astype(i32)
    blocks = near_far(
        keep, live, where, misc, queries, keys, values, halo_kv, glob, rand
    )
    return pack(blocks, packs, misc[0, 2], count, blk_dev, len(caps), choices)


def solution(mesh):
    in_specs = (
        P("seq", "head"),
        P("seq", "head"),
        P("seq", "head"),
        P("head", "seq", None),
        P("head", "seq", None),
        P("seq"),
    )
    out_specs = P("seq", "head")
    return jax.shard_map(body, mesh=mesh, in_specs=in_specs, out_specs=out_specs, check_vma=False)
```

profile of v0, /device:TPU:0, one launch (start us, length us, event | category | flops | bytes accessed | tf_op | source)
XLA Modules:
  0.0 361.4 jit_solution(15330060516340111313)
XLA Ops:
  0.0 0.7 broadcast_compare_fusion
  0.7 0.7 add_select_fusion
  1.4 0.1 copy.26
  1.5 0.1 copy.27
  1.6 0.7 pad.3.clone
  2.3 0.7 reshape.17
  3.0 7.3 %all-to-all-start = ((s32[32,1,256]{2,1,0:T(1,128)}), s32[32,1,256]{2,1,0:T(1,128)S(1)}, u32[]{:S(2)}, u32[]{:S(2)}) async-start(s32[32,1,256]{2,1,0:T(1,128)} %reshape.17), calls=%async_computation | async-start | bytes 65536 | tf_op jit(solution)/shard_map/all_to_all | solution.py:1157
  10.4 0.6 add_convert_fusion.live_ref
  11.0 6.6 %all-to-all-done = s32[32,1,256]{2,1,0:T(1,128)S(1)} async-done(((s32[32,1,256]{2,1,0:T(1,128)}), s32[32,1,256]{2,1,0:T(1,128)S(1)}, u32[]{:S(2)}, u32[]{:S(2)}) %all-to-all-start) | async-done | bytes 32800 | tf_op jit(solution)/shard_map/all_to_all | solution.py:1157
  17.6 0.5 broadcast.9
  18.1 0.7 reduce
  18.9 0.7 reshape.18
  19.6 4.2 %shard_map.81 = (s32[8,128]{1,0:T(8,128)S(1)}, s32[8,128]{1,0:T(8,128)}, s32[8,128]{1,0:T(8,128)}, s32[8,128]{1,0:T(8,128)S(1)}) custom-call(s32[256,32]{1,0:T(8,128)} %bitcast.7), custom_call_target="tpu_custom_call" | custom-call | tf_op jit(solution)/shard_map/pallas_call | solution.py:1112
  23.8 1.4 fusion
  25.9 211.0 %conditional.2 = ((bf16[312,256,128]{2,1,0:T(8,128)(2,1)}, bf16[2,256,1024]{2,1,0:T(8,128)(2,1)S(1)}, bf16[2,256,1024]{2,1,0:T(8,128)(2,1)})) conditional(s32[]{:T(128)} %bitcast.4, (s32[8,128]{1,0:T(8,128)S(1)}, bf16[1024,1024]{1,0:T(8,128)(2,1)}, bf16[1024,1024]{1,0:T(8,128)(2,1)}) %tuple.83, ...), branch_computations={%region_0.1_spmd, %region_1.2_spmd, %region_2.3_spmd, %region_3.4_... | conditional | bytes 8 | solution.py:1169
  25.9 210.7 %branch_4_fun.2 = (bf16[312,256,128]{2,1,0:T(8,128)(2,1)}, bf16[2,256,1024]{2,1,0:T(8,128)(2,1)S(1)}, bf16[2,256,1024]{2,1,0:T(8,128)(2,1)}) custom-call(s32[8,128]{1,0:T(8,128)S(1)} %get-tuple-element.152.tab, bf16[1024,1024]{1,0:T(8,128)(2,1)} %get-tuple-element.156.k_ref, bf16[1024,1024]{1,0:T(8,128)(2,1)} %get-tuple-element.158.v_ref), custom_call_target="tpu_custom_call" | custom-call | tf_op jit(solution)/shard_map/cond/branch_4_fun/pallas_call | solution.py:562
  236.8 26.4 %shard_map.82 = bf16[1024,1024]{1,0:T(8,128)(2,1)S(1)} custom-call(s32[8]{0:T(128)} %keep_ref.1, s32[2]{0:T(128)} %add_convert_fusion.live_ref, s32[8,128]{1,0:T(8,128)} %get-tuple-element.215.where_ref, s32[8,128]{1,0:T(8,128)} %get-tuple-element.213.used_ref, bf16[1024,1024]{1,0:T(8,128)(2,1)} %q_ref.1, bf16[1024,1024]{1,0:T(8,128)(2,1)} %k_ref.1, ...), custom_call_target="tpu_custom_call" | custom-call | tf_op jit(solution)/shard_map/pallas_call | solution.py:861
  263.8 94.5 %conditional.3 = (bf16[1024,1024]{1,0:T(8,128)(2,1)}) conditional(s32[]{:T(128)} %bitcast.1, (s32[8,128]{1,0:T(8,128)S(1)}, bf16[1024,1024]{1,0:T(8,128)(2,1)S(1)}) %tuple.84, (s32[8,128]{1,0:T(8,128)S(1)}, bf16[1024,1024]{1,0:T(8,128)(2,1)S(1)}) %tuple.84, (s32[8,128]{1,0:T(8,128)S(1)}, ...), branch_computations={%region_9.10_spmd, %region_10.11_spmd, %region_11.12_spmd, %region... | conditional | bytes 8 | solution.py:776
  263.9 94.4 %branch_8_fun.3 = bf16[1024,1024]{1,0:T(8,128)(2,1)} custom-call(s32[8,128]{1,0:T(8,128)S(1)} %get-tuple-element.188.table, bf16[1024,1024]{1,0:T(8,128)(2,1)S(1)} %get-tuple-element.189.in_ref), custom_call_target="tpu_custom_call" | custom-call | tf_op jit(solution)/shard_map/cond/branch_8_fun/pallas_call | solution.py:733
  358.3 3.1 copy.73
  (3 shorter events, 0.0 us)
Async XLA Ops:
  3.0 14.6 %all-to-all-start = ((s32[32,1,256]{2,1,0:T(1,128)}), s32[32,1,256]{2,1,0:T(1,128)S(1)}, u32[]{:S(2)}, u32[]{:S(2)}) async-start(s32[32,1,256]{2,1,0:T(1,128)} %reshape.17), calls=%async_computation | async-start | bytes 65536 | tf_op jit(solution)/shard_map/all_to_all | solution.py:1157
where the time goes:
time: 359 us; the launch traced here: 361 us
  Pallas kernels  336 us (94%)
  local copies, waits for them, and re-layouts  7.36 us (2%)
  starting transfers between devices  7.33 us (2%)
  waiting for transfers between devices  6.6 us (2%)
    pallas_call x1, Pallas kernels, exchange(): pl.pallas_call(functools.partial(exchange_kernel, count, cz, cx, blk_dev)...  211 us
    pallas_call x1, Pallas kernels, settled(): pl.pallas_call(functools.partial(settle_kernel, count, caps, cr, cx, blk_...  94.4 us
    pallas_call x1, Pallas kernels, near_far(): pl.pallas_call(functools.partial(near_far_kernel, blk_dev), out_shape=jax...  26.4 us
    all_to_all x1, starting transfers between devices, body(): lax.all_to_all(note, ('seq', 'head'), split_axis=0, concat_axis=0, tiled=...  7.33 us
  transfers between devices with their start and end apart: 1, of which 1 were waited for; matrix products, arithmetic and copies ran while one was open for 0% of the time, Pallas kernels for 0%

commit v1 on v0

--- a/solution.py
+++ b/solution.py
@@ -340,14 +340,13 @@
 
 def exchange_kernel(
     count, cz, cx, blk_dev, tab, k_ref, v_ref,
-    rand_ref, halo_ref, glob_ref, home, zs, zr, xs, own,
-    z_send, z_recv, x_send, x_recv, h_send, h_recv, g_send, g_recv, l_sem,
+    rand_ref, home, zs, zr, xs, own,
+    z_send, z_recv, x_send, x_recv, l_sem,
 ):
     planes = count // 2
     me = lax.axis_index("seq")
     plane, side = me // 2, me % 2
     mate = plane * 2 + 1 - side
-    tok = k_ref.shape[0]
     head_dev = k_ref.shape[1] // DH
     barrier = pltpu.get_barrier_semaphore()
     for step in range(1, count):
@@ -363,68 +362,7 @@
             device_id={"seq": peer}, device_id_type=pl.DeviceIdType.MESH,
         )
 
-    tables = (k_ref, v_ref)
     low, high = pl.ds(0, B), pl.ds(B, B)
-    first, last = pl.ds(0, B), pl.ds(tok - B, B)
-    after = jnp.minimum(me + 1, count - 1)
-    before = jnp.maximum(me - 1, 0)
-    ups = [
-        remote(tables[i].at[last], halo_ref.at[i, low], h_send.at[i], h_recv.at[i], after)
-        for i in range(2)
-    ]
-    downs = [
-        remote(tables[i].at[first], halo_ref.at[i, high], h_send.at[2 + i], h_recv.at[2 + i], before)
-        for i in range(2)
-    ]
-    local = [
-        pltpu.make_async_copy(tables[i].at[pl.ds(0, G * B)], glob_ref.at[i], l_sem.at[i])
-        for i in range(2)
-    ]
-    item = glob_ref.at[side]
-    chain = remote(item, item, g_send.at[0], g_recv.at[0], jnp.minimum(me + 2, count - 1))
-    swap = remote(item, item, g_send.at[1], g_recv.at[1], mate)
-    extra = remote(glob_ref.at[1], glob_ref.at[1], g_send.at[2], g_recv.at[0], mate)
-
-    @pl.when(me == 0)
-    def _():
-        for c in local:
-            c.start()
-        for c in local:
-            c.wait()
-        chain.start()
-        extra.start()
-        swap.start()
-
-    def pass_on():
-        @pl.when(me > 0)
-        def _():
-            chain.wait_recv()
-
-            @pl.when(plane < planes - 1)
-            def _():
-                chain.start()
-
-            @pl.when(me > 1)
-            def _():
-                swap.start()
-
-    @pl.when(me < count - 1)
-    def _():
-        for c in ups:
-            c.start()
-
-    @pl.when(me > 0)
-    def _():
-        for c in downs:
-            c.start()
-
-    @pl.when(me == 0)
-    def _():
-        halo_ref[:, low, :] = jnp.zeros((2, B, k_ref.shape[1]), k_ref.dtype)
-
-    @pl.when(me == count - 1)
-    def _():
-        halo_ref[:, high, :] = jnp.zeros((2, B, k_ref.shape[1]), k_ref.dtype)
 
     def load_home(block, carry):
         rows = pl.ds(pl.multiple_of(block * B, B), B)
@@ -480,10 +418,8 @@
         @pl.when(plane == q)
         def _(q=q):
             order = goals(q)
-            for n, d in enumerate(order):
+            for d in order:
                 z_copies[d].start()
-                if n == 0 and q == 0:
-                    pass_on()
 
     x_copies[0].start()
     from_slots(own, home, tab, 2 * planes - 1, cx)
@@ -507,42 +443,8 @@
     for q in range(planes):
         @pl.when(plane == q)
         def _(q=q):
-            for n, d in enumerate(sources(q)):
+            for d in sources(q):
                 forward(d)
-                if n == 0 and 0 < q < planes // 2:
-                    pass_on()
-            if q >= planes // 2:
-                pass_on()
-
-    @pl.when(me > 0)
-    def _():
-        swap.wait_recv()
-
-    @pl.when(plane < planes - 1)
-    def _():
-        chain.wait_send()
-
-    @pl.when(me == 0)
-    def _():
-        extra.wait_send()
-
-    @pl.when(me != 1)
-    def _():
-        swap.wait_send()
-
-    @pl.when(me < count - 1)
-    def _():
-        for c in ups:
-            c.wait_send()
-        for c in downs:
-            c.wait_recv()
-
-    @pl.when(me > 0)
-    def _():
-        for c in downs:
-            c.wait_send()
-        for c in ups:
-            c.wait_recv()
 
     keep_own.wait()
     for d in deltas:
@@ -561,13 +463,9 @@
     dma = pltpu.SemaphoreType.DMA
     return pl.pallas_call(
         functools.partial(exchange_kernel, count, cz, cx, blk_dev),
-        out_shape=(
-            jax.ShapeDtypeStruct((slots, *TILE), dtype),
-            jax.ShapeDtypeStruct((2, 2 * B, width), dtype),
-            jax.ShapeDtypeStruct((2, G * B, width), dtype),
-        ),
+        out_shape=jax.ShapeDtypeStruct((slots, *TILE), dtype),
         in_specs=[smem, vmem, vmem],
-        out_specs=(pl.BlockSpec(memory_space=pl.ANY), vmem, vmem),
+        out_specs=pl.BlockSpec(memory_space=pl.ANY),
         scratch_shapes=[
             pltpu.VMEM((tok // B * (width // DH), *TILE), dtype),
             [pltpu.VMEM((cz, *TILE), dtype) for _ in range(planes - 1)],
@@ -576,7 +474,7 @@
             pltpu.VMEM((cx, *TILE), dtype),
             dma((planes - 1,)), dma((planes - 1,)),
             dma((planes,)), dma((planes,)),
-            dma((4,)), dma((4,)), dma((3,)), dma((2,)), dma((2 + planes,)),
+            dma((2 + planes,)),
         ],
         compiler_params=pltpu.CompilerParams(
             collective_id=level, has_side_effects=True,
@@ -764,7 +662,12 @@
         for r in (half // 2, half)
         if abs(f - t) < 2 or t == half
     ]
-    choices = sorted(choices) + [(0, (blk_dev,) * (planes - 1), blk_dev, blk_dev)]
+    choices = sorted(choices) + [
+        (0, pad(half + 1, half + 1), few, few + 1),
+        (0, pad(few + 1, half + 1), half // 2, few + 1),
+        (0, ((few + 1, few) + (1,) * planes)[: planes - 1], few, few + 1),
+        (0, (blk_dev,) * (planes - 1), blk_dev, blk_dev),
+    ]
     return [limits for _, *limits in choices]
 
 
@@ -882,14 +785,128 @@
 
 
 def plan_kernel(
-    count, head_count, blk_dev, most, caps, choices, note_ref, tab_ref, where_ref, misc_ref, pack_ref,
-    need_ref, want_ref, slot_ref, both_ref, both_slot_ref,
+    count, head_count, blk_dev, caps, choices, own_ref, k_ref, v_ref,
+    tab_ref, where_ref, misc_ref, pack_ref, halo_ref, glob_ref,
+    note_ref, need_ref, want_ref, slot_ref, both_ref, both_slot_ref,
+    n_send, n_recv, h_send, h_recv, g_send, g_recv, s_send, s_recv, e_send, l_sem,
 ):
     i32, f32, bf16 = jnp.int32, jnp.float32, jnp.bfloat16
     planes = count // 2
     me, group = lax.axis_index("seq"), lax.axis_index("head")
     plane, side = me // 2, me % 2
     mate = me + 1 - 2 * side
+    tall = own_ref.shape[0]
+    everyone = count * head_count
+    here_id = me * head_count + group
+    barrier = pltpu.get_barrier_semaphore()
+
+    def device(step):
+        other = lax.rem(here_id + step, everyone)
+        return {"seq": other // head_count, "head": lax.rem(other, head_count)}
+
+    for step in range(1, everyone):
+        pl.semaphore_signal(
+            barrier, inc=1, device_id=device(step), device_id_type=pl.DeviceIdType.MESH
+        )
+    pl.semaphore_wait(barrier, everyone - 1)
+
+    def remote(src, dst, send, recv, peer):
+        return pltpu.make_async_remote_copy(
+            src_ref=src, dst_ref=dst, send_sem=send, recv_sem=recv,
+            device_id=peer, device_id_type=pl.DeviceIdType.MESH,
+        )
+
+    slot_rows = pl.ds(pl.multiple_of(here_id * tall, tall), tall)
+    notices = [
+        remote(
+            own_ref, note_ref.at[slot_rows], n_send.at[step - 1], n_recv.at[step - 1], device(step)
+        )
+        for step in range(1, everyone)
+    ]
+    for c in notices:
+        c.start()
+    note_ref[slot_rows, :] = own_ref[...]
+
+    tables = (k_ref, v_ref)
+    low, high = pl.ds(0, B), pl.ds(B, B)
+    tok, width = k_ref.shape
+    after, before = jnp.minimum(me + 1, count - 1), jnp.maximum(me - 1, 0)
+    ups = [
+        remote(
+            tables[i].at[pl.ds(tok - B, B)], halo_ref.at[i, low],
+            h_send.at[i], h_recv.at[i], {"seq": after},
+        )
+        for i in range(2)
+    ]
+    downs = [
+        remote(
+            tables[i].at[pl.ds(0, B)], halo_ref.at[i, high],
+            h_send.at[2 + i], h_recv.at[2 + i], {"seq": before},
+        )
+        for i in range(2)
+    ]
+    local = [
+        pltpu.make_async_copy(tables[i].at[pl.ds(0, G * B)], glob_ref.at[i], l_sem.at[i])
+        for i in range(2)
+    ]
+    onto = {"seq": jnp.minimum(me + 2, count - 1)}
+    chain, swap, extra = [], [], []
+    for n in range(PIECES):
+        part = pl.ds(n * (width // PIECES), width // PIECES)
+        item, other = glob_ref.at[side, :, part], glob_ref.at[1, :, part]
+        chain.append(remote(item, item, g_send.at[n], g_recv.at[n], onto))
+        swap.append(remote(item, item, s_send.at[n], s_recv.at[n], {"seq": mate}))
+        extra.append(remote(other, other, e_send.at[n], g_recv.at[n], {"seq": mate}))
+
+    @pl.when(me == 0)
+    def _():
+        for c in local:
+            c.start()
+        for c in local:
+            c.wait()
+        for n in range(PIECES):
+            chain[n].start()
+            extra[n].start()
+        for c in swap:
+            c.start()
+
+    @pl.when(me < count - 1)
+    def _():
+        for c in ups:
+            c.start()
+
+    @pl.when(me > 0)
+    def _():
+        for c in downs:
+            c.start()
+
+    @pl.when(me == 0)
+    def _():
+        halo_ref[:, low, :] = jnp.zeros((2, B, width), k_ref.dtype)
+
+    @pl.when(me == count - 1)
+    def _():
+        halo_ref[:, high, :] = jnp.zeros((2, B, width), k_ref.dtype)
+
+    def pass_on():
+        for n in range(PIECES):
+            chain[n].wait_recv()
+
+            @pl.when(plane < planes - 1)
+            def _(n=n):
+                chain[n].start()
+
+            @pl.when(me > 1)
+            def _(n=n):
+                swap[n].start()
+
+    for c in notices:
+        c.wait_recv()
+
+    @pl.when(jnp.logical_and(me > 0, plane <= 1))
+    def _():
+        pass_on()
+
     rows, lanes = note_ref.shape[0], tab_ref.shape[1]
     head_dev = rows // (count * head_count)
     count_req = blk_dev * R
@@ -1099,29 +1116,81 @@
         spot8 == 0, level, jnp.where(spot8 == 1, used, jnp.where(spot8 == 2, pick, 0))
     )
 
-
-def plan(note, count, head_count, blk_dev, most, caps, choices):
-    rows = note.shape[0]
+    @pl.when(plane > 1)
+    def _():
+        pass_on()
+
+    @pl.when(me > 0)
+    def _():
+        for c in swap:
+            c.wait_recv()
+
+    @pl.when(plane < planes - 1)
+    def _():
+        for c in chain:
+            c.wait_send()
+
+    @pl.when(me == 0)
+    def _():
+        for c in extra:
+            c.wait_send()
+
+    @pl.when(me != 1)
+    def _():
+        for c in swap:
+            c.wait_send()
+
+    @pl.when(me < count - 1)
+    def _():
+        for c in ups:
+            c.wait_send()
+        for c in downs:
+            c.wait_recv()
+
+    @pl.when(me > 0)
+    def _():
+        for c in downs:
+            c.wait_send()
+        for c in ups:
+            c.wait_recv()
+
+    for c in notices:
+        c.wait_send()
+
+
+def plan(note, keys, values, count, head_count, blk_dev, caps, choices, number):
+    head_dev, width = note.shape[0], keys.shape[1]
+    everyone = count * head_count
+    rows = everyone * head_dev
     planes = count // 2
-    head_dev = rows // (count * head_count)
     lanes = max(128, count * blk_dev)
     i32, f32 = jnp.int32, jnp.float32
     tabs = -(-2 * planes // 8) * 8
     packs = -(-(planes + max(planes // 2 - 1, 1) + 3) // 8) * 8
-    shape = jax.ShapeDtypeStruct
+    shape, dma = jax.ShapeDtypeStruct, pltpu.SemaphoreType.DMA
+    vmem, anywhere = pl.BlockSpec(memory_space=pltpu.VMEM), pl.BlockSpec(memory_space=pl.ANY)
     return pl.pallas_call(
-        functools.partial(plan_kernel, count, head_count, blk_dev, most, caps, choices),
+        functools.partial(plan_kernel, count, head_count, blk_dev, caps, choices),
         out_shape=(
             shape((tabs, lanes), i32), shape((head_dev, lanes), i32),
             shape((8, lanes), i32), shape((packs, lanes), i32),
+            shape((2, 2 * B, width), keys.dtype), shape((2, G * B, width), keys.dtype),
         ),
+        in_specs=[vmem, anywhere, anywhere],
+        out_specs=(vmem,) * 6,
         scratch_shapes=[
+            pltpu.VMEM((rows, note.shape[1]), i32),
             pltpu.VMEM((rows, lanes), f32),
             pltpu.VMEM((count * head_dev, lanes), f32), pltpu.VMEM((count * head_dev, lanes), f32),
             pltpu.VMEM((planes * head_dev, lanes), f32), pltpu.VMEM((planes * head_dev, lanes), f32),
+            dma((everyone - 1,)), dma((everyone - 1,)), dma((4,)), dma((4,)),
+            dma((PIECES,)), dma((PIECES,)), dma((PIECES,)), dma((PIECES,)), dma((PIECES,)), dma((2,)),
         ],
-        compiler_params=SMALL,
-    )(note)
+        compiler_params=pltpu.CompilerParams(
+            collective_id=number, has_side_effects=True,
+            vmem_limit_bytes=60 * 1024 * 1024,
+        ),
+    )(note, keys, values)
 
 
 def levels(tiles, most):
@@ -1152,12 +1221,13 @@
     i32 = jnp.int32
     code = random_holder * blk_dev + random_offset
     code = jnp.where((keep > 0)[None, :, None], code, -1).reshape(head_dev, count_req)
+    wide = -(-(count_req + blk_dev) // 128) * 128
     note = jnp.concatenate([code, jnp.broadcast_to(keep[None], (head_dev, blk_dev))], axis=1)
-    note = jnp.broadcast_to(note, (count * head_count,) + note.shape)
-    table = lax.all_to_all(note, ("seq", "head"), split_axis=0, concat_axis=0, tiled=True)
-    table = table.reshape(count * head_count * head_dev, count_req + blk_dev)
+    note = jnp.pad(note, ((0, 0), (0, wide - count_req - blk_dev)), constant_values=-1)
     caps, choices = levels(tiles, most), settle_levels(planes, blk_dev)
-    tab, where, misc, packs = plan(table, count, head_count, blk_dev, most, caps, choices)
+    tab, where, misc, packs, halo_kv, glob = plan(
+        note, keys, values, count, head_count, blk_dev, caps, choices, len(caps) + len(choices)
+    )
 
     slots_all = -(-max((planes - 1) * c[0] + (planes + 1) * c[1] for c in caps) // CHUNK) * CHUNK
     def exchanged(number, caps):
@@ -1166,7 +1236,7 @@
 
         return run
 
-    rand, halo_kv, glob = lax.switch(
+    rand = lax.switch(
         misc[0, 0], [exchanged(n, c) for n, c in enumerate(caps)], tab, keys, values
     )
 

time: 359 us -> 346 us (0.964); the launches traced: 361 us -> 344 us
  starting transfers between devices: 7.33 us -> 0 us
  waiting for transfers between devices: 6.6 us -> 0 us
    pallas_call x1, Pallas kernels: 4.21 us -> 57.5 us  [plan(): pl.pallas_call(functools.partial(plan_kernel, count, head_count, blk_dev,...]
    pallas_call x1, Pallas kernels: 211 us -> 184 us  [exchange(): pl.pallas_call(functools.partial(exchange_kernel, count, cz, cx, blk_dev)...]
    pallas_call x1, Pallas kernels: 94.4 us -> 71.4 us  [settled(): pl.pallas_call(functools.partial(settle_kernel, count, caps, cr, cx, blk_...]
    all_to_all x1 -> x0, starting transfers between devices: 7.33 us -> none  [body(): lax.all_to_all(note, ('seq', 'head'), split_axis=0, concat_axis=0, tiled=...]
    all_to_all x1 -> x0, waiting for transfers between devices: 6.6 us -> none  [body(): lax.all_to_all(note, ('seq', 'head'), split_axis=0, concat_axis=0, tiled=...]
    pallas_call x1, Pallas kernels: 26.4 us -> 21.6 us  [near_far(): pl.pallas_call(functools.partial(near_far_kernel, blk_dev), out_shape=jax...]
  transfers between devices with their start and end apart: 1 -> 0, of which waited for: 1 -> 0; matrix products, arithmetic and copies ran while one was open for 0% -> 0% of each run, Pallas kernels for 0% -> 0%
where the time goes in v1:
time: 346 us; the launch traced here: 344 us
  Pallas kernels  334 us (97%)
  local copies, waits for them, and re-layouts  5.93 us (2%)
    pallas_call x1, Pallas kernels, exchange(): pl.pallas_call(functools.partial(exchange_kernel, count, cz, cx, blk_dev)...  184 us
    pallas_call x1, Pallas kernels, settled(): pl.pallas_call(functools.partial(settle_kernel, count, caps, cr, cx, blk_...  71.4 us
    pallas_call x1, Pallas kernels, plan(): pl.pallas_call(functools.partial(plan_kernel, count, head_count, blk_dev,...  57.5 us
    pallas_call x1, Pallas kernels, near_far(): pl.pallas_call(functools.partial(near_far_kernel, blk_dev), out_shape=jax...  21.6 us

profile of v1, /device:TPU:0, one launch (start us, length us, event | category | flops | bytes accessed | tf_op | source)
XLA Modules:
  0.0 344.3 jit_solution(7362432691828834173)
XLA Ops:
  0.0 0.7 broadcast_compare_fusion
  0.7 0.7 add_select_fusion
  1.4 0.1 copy.28
  1.5 0.1 copy.29
  1.6 0.7 pad.8.clone
  2.3 0.6 pad.4.own_ref
  2.9 0.0 copy-start
  2.9 57.5 %shard_map.84 = (s32[8,128]{1,0:T(8,128)S(1)}, s32[8,128]{1,0:T(8,128)}, s32[8,128]{1,0:T(8,128)}, s32[8,128]{1,0:T(8,128)S(1)}, bf16[2,256,1024]{2,1,0:T(8,128)(2,1)}, /*index=5*/bf16[2,256,1024]{2,1,0:T(8,128)(2,1)}) custom-call(s32[8,128]{1,0:T(8,128)} %pad.4.own_ref, bf16[1024,1024]{1,0:T(8,128)(2,1)} %k_ref.3, bf16[1024,1024]{1,0:T(8,128)(2,1)} %v_ref.3), custom_call_target="tpu_custom_call" | custom-call | tf_op jit(solution)/shard_map/pallas_call | solution.py:1172
  60.4 1.4 fusion
  62.4 0.0 copy-done
  62.5 184.0 %conditional.2 = (bf16[312,256,128]{2,1,0:T(8,128)(2,1)}) conditional(s32[]{:T(128)} %bitcast.3, (s32[8,128]{1,0:T(8,128)S(1)}, bf16[1024,1024]{1,0:T(8,128)(2,1)S(1)}, bf16[1024,1024]{1,0:T(8,128)(2,1)}) %tuple.144, (s32[8,128]{1,0:T(8,128)S(1)}, bf16[1024,1024]{1,0:T(8,128)(2,1)S(1)}, ...), branch_computations={%region_0.1_spmd, %region_1.2_spmd, %region_2.3_spmd, %region_3.4_... | conditional | bytes 8 | solution.py:1239
  62.5 183.9 %branch_2_fun.2 = bf16[312,256,128]{2,1,0:T(8,128)(2,1)} custom-call(s32[8,128]{1,0:T(8,128)S(1)} %get-tuple-element.156.tab, bf16[1024,1024]{1,0:T(8,128)(2,1)S(1)} %get-tuple-element.157.k_ref, bf16[1024,1024]{1,0:T(8,128)(2,1)} %get-tuple-element.158.v_ref), custom_call_target="tpu_custom_call" | custom-call | tf_op jit(solution)/shard_map/cond/branch_2_fun/pallas_call | solution.py:464
  246.4 0.7 add_convert_fusion.live_ref
  247.1 21.6 %shard_map.85 = bf16[1024,1024]{1,0:T(8,128)(2,1)S(1)} custom-call(s32[8]{0:T(128)} %keep_ref.1, s32[2]{0:T(128)} %add_convert_fusion.live_ref, s32[8,128]{1,0:T(8,128)} %get-tuple-element.245.where_ref, s32[8,128]{1,0:T(8,128)} %get-tuple-element.243.used_ref, bf16[1024,1024]{1,0:T(8,128)(2,1)} %q_ref.1, bf16[1024,1024]{1,0:T(8,128)(2,1)} %k_ref.3, ...), custom_call_target="tpu_custom_call" | custom-call | tf_op jit(solution)/shard_map/pallas_call | solution.py:764
  269.3 71.9 %conditional.3 = (bf16[1024,1024]{1,0:T(8,128)(2,1)}) conditional(s32[]{:T(128)} %bitcast, (s32[8,128]{1,0:T(8,128)S(1)}, bf16[1024,1024]{1,0:T(8,128)(2,1)S(1)}) %tuple.93, (s32[8,128]{1,0:T(8,128)S(1)}, bf16[1024,1024]{1,0:T(8,128)(2,1)S(1)}) %tuple.93, (s32[8,128]{1,0:T(8,128)S(1)}, ...), branch_computations={%region_9.10_spmd, %region_10.11_spmd, %region_11.12_spmd, %region... | conditional | bytes 8 | solution.py:679
  269.4 71.4 %branch_1_fun.3 = bf16[1024,1024]{1,0:T(8,128)(2,1)} custom-call(s32[8,128]{1,0:T(8,128)S(1)} %get-tuple-element.199.table, bf16[1024,1024]{1,0:T(8,128)(2,1)S(1)} %get-tuple-element.200.in_ref), custom_call_target="tpu_custom_call" | custom-call | tf_op jit(solution)/shard_map/cond/branch_1_fun/pallas_call | solution.py:631
  341.2 3.1 copy.60
  (2 shorter events, 0.0 us)
Async XLA Ops:
  2.9 59.6 %copy-start = (bf16[1024,1024]{1,0:T(8,128)(2,1)S(1)}, bf16[1024,1024]{1,0:T(8,128)(2,1)}, u32[]{:S(2)}) copy-start(bf16[1024,1024]{1,0:T(8,128)(2,1)} %k_ref.3) | copy-start | bytes 6291460
